TPU v7x, 32 devices: a whole 2x2x4 slice. The times are simulated.
32 devices in a mesh: rows: 8 (over z, x), width: 4 (over y, core).
Axes of the slice: x: 2, y: 2, z: 4, core: 2. Of those that a mesh axis runs over, the one named last changes fastest.
Arguments:
- weight_gate: float32 [2560, 9728], P('rows', 'width'), may hold values from -0.15625 to 0.15625
- moment_gate: float32 [2560, 9728], P('rows', 'width'), may hold values from -6 to 6
- square_gate: float32 [2560, 9728], P('rows', 'width'), may hold values from 0.1 to 10
- weight_up: float32 [2560, 9728], P('rows', 'width'), may hold values from -0.15625 to 0.15625
- moment_up: float32 [2560, 9728], P('rows', 'width'), may hold values from -6 to 6
- square_up: float32 [2560, 9728], P('rows', 'width'), may hold values from 0.1 to 10
- norm_gain: float32 [2560], P('rows'), may hold values from 0.25 to 1.75
Outputs:
- ready_gate: bfloat16 [2560, 9728], P(None, 'width')
- ready_up: bfloat16 [2560, 9728], P(None, 'width')
- column_gate: float32 [9728], P('width')
- column_up: float32 [9728], P('width')
All inputs are finite; a program needn't handle non-finite values.
Results may differ from a plain program's by a relative error of at most 0.0004.
Values may be sent and summed in bfloat16 or wider, within the bound.
A program may use at most 128 MiB of HBM per device.

v0:
```python
import functools

import jax
import jax.numpy as jnp
from jax import lax
from jax.experimental import pallas as pl
from jax.experimental.pallas import tpu as pltpu
from jax.sharding import PartitionSpec as P

learn_rate = 0.02
decay_rate = 0.1
tiny_value = 1e-08
lanes = 128
vmem_bytes = 67043328
block_rows = 16
MESH = pl.DeviceIdType.MESH


def column_cuts(columns):
    tiles = columns // lanes
    first = max(1, tiles // 9)
    rest = tiles - first
    sizes = [first] + [rest // 3 + (1 if i < rest % 3 else 0) for i in range(3)]
    cuts, at = [], 0
    for size in sizes:
        if size:
            cuts.append((at * lanes, size * lanes))
        at += size
    return cuts


def gather_kernel(
    n, gain_ref, wg, mg, sg, wu, mu, su, out_gate, out_up, col_gate, col_up,
    values, moments, squares, parts, in_sem, part_send, part_recv, send_sem, recv_sem,
):
    me = lax.axis_index("rows")
    w = lax.axis_index("width")
    length = n // 2
    place, side = me // 2, me % 2
    mate = place + 1 - 2 * (place % 2)
    rows, columns = wg.shape
    cuts = column_cuts(columns)
    half = len(cuts)
    chunks = [(t, at, size) for t in range(2) for at, size in cuts]
    sources = ((wg, mg, sg), (wu, mu, su))
    outs = (out_gate, out_up)
    cols = (col_gate, col_up)

    def fetch(k):
        t, at, size = chunks[k]
        return [
            pltpu.make_async_copy(src.at[:, pl.ds(at, size)], dst.at[t, :, pl.ds(at, size)], in_sem.at[i, k])
            for i, (src, dst) in enumerate(zip(sources[t], (values, moments, squares)))
        ]

    for k in range(len(chunks)):
        for copy in fetch(k):
            copy.start()

    barrier = pltpu.get_barrier_semaphore()

    def greet(i, carry):
        peer = lax.rem(me + i, n)
        pl.semaphore_signal(barrier, inc=1, device_id=(peer, w), device_id_type=MESH)
        return carry

    lax.fori_loop(1, n, greet, 0)

    def part_copy(k, peer):
        t, at, size = chunks[k]
        here = parts.at[me, t, :, pl.ds(at, size)]
        return pltpu.make_async_remote_copy(
            src_ref=here, dst_ref=here, send_sem=part_send.at[k], recv_sem=part_recv.at[k],
            device_id=(peer, w), device_id_type=MESH,
        )

    def compute(k):
        t, at, size = chunks[k]
        for copy in fetch(k):
            copy.wait()

        def step(b, total):
            here = pl.ds(pl.multiple_of(b * block_rows, block_rows), block_rows)
            there = pl.ds(at, size)
            weight = values[t, here, there]
            latest = weight - learn_rate * (
                moments[t, here, there] / (jnp.sqrt(squares[t, here, there]) + tiny_value) + decay_rate * weight
            )
            gain = jnp.concatenate([gain_ref[here, :]] * (size // lanes), axis=1)
            gained = latest * gain
            values[t, here, there] = gained
            squared = gained * gained
            for r in range(0, block_rows, 8):
                total = total + squared[r : r + 8]
            return total

        total = lax.fori_loop(0, rows // block_rows, step, jnp.zeros((8, size), jnp.float32))
        parts[me, t, :, pl.ds(at, size)] = jnp.sum(total, axis=0, keepdims=True)

    def share_parts(k):
        def send(i, carry):
            part_copy(k, lax.rem(me + i, n)).start()
            return carry

        lax.fori_loop(1, n, send, 0)

    def part_bytes(k, sem):
        t, at, size = chunks[k]
        refs = parts.at[pl.ds(0, n - 1), t, :, pl.ds(at, size)]
        return pltpu.make_async_copy(refs, refs, sem)

    def block(share, k):
        t, at, size = chunks[k]
        start = pl.multiple_of(share * rows, rows)
        return outs[t].at[pl.ds(start, rows), pl.ds(at, size)]

    def push(link, slot, share, k):
        there = ((place - 1) * 2 + side, (place + 1) * 2 + side, place * 2 + 1 - side)[link]
        here = block(share, k)
        return pltpu.make_async_remote_copy(
            src_ref=here, dst_ref=here,
            send_sem=send_sem.at[link, slot, k], recv_sem=recv_sem.at[share, k],
            device_id=(there, w), device_id_type=MESH,
        )

    def arrived(share, k):
        here = block(share, k)
        pltpu.make_async_copy(here, here, recv_sem.at[share, k]).wait()

    def finish(k):
        t, at, size = chunks[k]
        part_bytes(k, part_recv.at[k]).wait()
        total = parts[0, t, :, pl.ds(at, size)]
        for i in range(1, n):
            total = total + parts[i, t, :, pl.ds(at, size)]
        scale = jnp.sqrt(total)
        cols[t][:, pl.ds(at, size)] = scale

        def step(b, carry):
            here = pl.ds(pl.multiple_of(b * block_rows, block_rows), block_rows)
            there = pl.ds(pl.multiple_of(me * rows + b * block_rows, block_rows), block_rows)
            outs[t][there, pl.ds(at, size)] = (values[t, here, pl.ds(at, size)] / scale).astype(jnp.bfloat16)
            return carry

        lax.fori_loop(0, rows // block_rows, step, 0)

    def send_own(k):
        @pl.when(place > 0)
        def _():
            push(0, 0, me, k).start()

        @pl.when(place < length - 1)
        def _():
            push(1, 0, me, k).start()

        push(2, 0, me, k).start()

    compute(0)
    pl.semaphore_wait(barrier, n - 1)
    share_parts(0)
    for k in range(len(chunks)):
        if k + 1 < len(chunks):
            compute(k + 1)
            share_parts(k + 1)
        finish(k)
        send_own(k)

    def spread(d, carry):
        for k in range(len(chunks)):
            @pl.when(place + d < length)
            def _():
                share = (place + d) * 2 + side
                arrived(share, k)

                @pl.when(place > 0)
                def _():
                    push(0, d, share, k).start()

                if k < half:
                    push(2, d, share, k).start()
                else:
                    @pl.when(place + d != mate)
                    def _():
                        push(2, d, share, k).start()

            @pl.when(place - d >= 0)
            def _():
                share = (place - d) * 2 + side
                arrived(share, k)

                @pl.when(place < length - 1)
                def _():
                    push(1, d, share, k).start()

                if k < half:
                    push(2, length + d, share, k).start()
                else:
                    @pl.when(place - d != mate)
                    def _():
                        push(2, length + d, share, k).start()

        return carry

    def extra(action):
        share = place * 2 + 1 - side
        for k in range(half, len(chunks)):
            if action == "start":
                arrived(share, k)

            @pl.when(mate < place)
            def _():
                copy = push(0, length, share, k)
                copy.start() if action == "start" else copy.wait_send()

            @pl.when(mate > place)
            def _():
                copy = push(1, length, share, k)
                copy.start() if action == "start" else copy.wait_send()

    middle = max(1, length // 2) + 1
    lax.fori_loop(1, middle, spread, 0)
    extra("start")
    lax.fori_loop(middle, length, spread, 0)

    def collect(q, carry):
        share = q * 2 + 1 - side
        for k in range(len(chunks)):
            if k < half:
                arrived(share, k)
            else:
                @pl.when(q != place)
                def _():
                    arrived(share, k)
        return carry

    lax.fori_loop(0, length, collect, 0)

    for k in range(len(chunks)):
        part_bytes(k, part_send.at[k]).wait()

        @pl.when(place > 0)
        def _():
            push(0, 0, me, k).wait_send()

        @pl.when(place < length - 1)
        def _():
            push(1, 0, me, k).wait_send()

        push(2, 0, me, k).wait_send()
    extra("wait")

    def drain(d, carry):
        for k in range(len(chunks)):
            @pl.when(place + d < length)
            def _():
                share = (place + d) * 2 + side

                @pl.when(place > 0)
                def _():
                    push(0, d, share, k).wait_send()

                if k < half:
                    push(2, d, share, k).wait_send()
                else:
                    @pl.when(place + d != mate)
                    def _():
                        push(2, d, share, k).wait_send()

            @pl.when(place - d >= 0)
            def _():
                share = (place - d) * 2 + side

                @pl.when(place < length - 1)
                def _():
                    push(1, d, share, k).wait_send()

                if k < half:
                    push(2, length + d, share, k).wait_send()
                else:
                    @pl.when(place - d != mate)
                    def _():
                        push(2, length + d, share, k).wait_send()

        return carry

    lax.fori_loop(1, length, drain, 0)


def write_kernel(pieces, gate, up, out_gate, out_up, sem):
    step = gate.shape[0] // pieces
    copies = [
        pltpu.make_async_copy(src.at[pl.ds(i * step, step)], dst.at[pl.ds(i * step, step)], sem.at[t, i])
        for i in range(pieces)
        for t, (src, dst) in enumerate(((gate, out_gate), (up, out_up)))
    ]
    for copy in copies:
        copy.start()
    for copy in copies:
        copy.wait()


def write_out(pieces, gate, up):
    vmem = pl.BlockSpec(memory_space=pltpu.VMEM)
    hbm = pl.BlockSpec(memory_space=pltpu.HBM)
    return pl.pallas_call(
        functools.partial(write_kernel, pieces),
        out_shape=[jax.ShapeDtypeStruct(a.shape, a.dtype) for a in (gate, up)],
        in_specs=[vmem, vmem],
        out_specs=[hbm, hbm],
        scratch_shapes=[pltpu.SemaphoreType.DMA((2, pieces))],
        compiler_params=pltpu.CompilerParams(vmem_limit_bytes=2**20),
        name="write_out",
    )(gate, up)


def per_device(n, weight_gate, moment_gate, square_gate, weight_up, moment_up, square_up, norm_gain):
    rows, columns = weight_gate.shape
    gain = jnp.broadcast_to(norm_gain[:, None], (rows, lanes))
    count = 2 * len(column_cuts(columns))
    vmem = pl.BlockSpec(memory_space=pltpu.VMEM)
    hbm = pl.BlockSpec(memory_space=pltpu.HBM)
    room = vmem_bytes - 2 * n * rows * columns * 2 - 3 * 2**19
    ready_gate, ready_up, column_gate, column_up = pl.pallas_call(
        functools.partial(gather_kernel, n),
        out_shape=(
            pltpu.VMEM((n * rows, columns), jnp.bfloat16),
            pltpu.VMEM((n * rows, columns), jnp.bfloat16),
            jax.ShapeDtypeStruct((1, columns), jnp.float32),
            jax.ShapeDtypeStruct((1, columns), jnp.float32),
        ),
        in_specs=[vmem] + [hbm] * 6,
        out_specs=(vmem, vmem, vmem, vmem),
        scratch_shapes=[
            pltpu.VMEM((2, rows, columns), jnp.float32),
            pltpu.VMEM((2, rows, columns), jnp.float32),
            pltpu.VMEM((2, rows, columns), jnp.float32),
            pltpu.VMEM((n, 2, 1, columns), jnp.float32),
            pltpu.SemaphoreType.DMA((3, count)),
            pltpu.SemaphoreType.DMA((count,)),
            pltpu.SemaphoreType.DMA((count,)),
            pltpu.SemaphoreType.DMA((3, n, count)),
            pltpu.SemaphoreType.DMA((n, count)),
        ],
        compiler_params=pltpu.CompilerParams(
            collective_id=0, has_side_effects=True, vmem_limit_bytes=room
        ),
        name="step_and_gather",
    )(gain, weight_gate, moment_gate, square_gate, weight_up, moment_up, square_up)
    ready_gate, ready_up = write_out(n, ready_gate, ready_up)
    return ready_gate, ready_up, column_gate.reshape(columns), column_up.reshape(columns)


def solution(mesh):
    split = P("rows", "width")
    return jax.shard_map(
        functools.partial(per_device, mesh.shape["rows"]),
        mesh=mesh,
        in_specs=(split,) * 6 + (P("rows"),),
        out_specs=(P(None, "width"), P(None, "width"), P("width"), P("width")),
        check_vma=False,
    )
```

profile of v0, /device:TPU:0, one launch (start us, length us, event | category | flops | bytes accessed | tf_op | source)
XLA Modules:
  0.0 261.5 jit_solution(3788356689067105910)
XLA Ops:
  0.6 1.5 broadcast_in_dim.2.gain_ref
  2.1 249.7 %step_and_gather.1 = (bf16[2560,2432]{1,0:T(8,128)(2,1)S(1)}, bf16[2560,2432]{1,0:T(8,128)(2,1)S(1)}, f32[1,2432]{1,0:T(1,128)}, f32[1,2432]{1,0:T(1,128)}) custom-call(f32[320,128]{1,0:T(8,128)} %broadcast_in_dim.2.gain_ref, f32[320,2432]{1,0:T(8,128)} %wg.1, f32[320,2432]{1,0:T(8,128)} %mg.1, f32[320,2432]{1,0:T(8,128)} %sg.1, f32[320,2432]{1,0:T(8,128)} %wu.1, ...), custom_call_target="tpu_custom_call" | custom-call | tf_op jit(solution)/shard_map/step_and_gather/pallas_call | solution.py:323
  251.8 0.0 copy-start.1
  251.8 0.0 copy-start
  251.8 8.4 %write_out.1 = (bf16[2560,2432]{1,0:T(8,128)(2,1)}, bf16[2560,2432]{1,0:T(8,128)(2,1)}) custom-call(bf16[2560,2432]{1,0:T(8,128)(2,1)S(1)} %get-tuple-element.10.gate, bf16[2560,2432]{1,0:T(8,128)(2,1)S(1)} %get-tuple-element.11.up), custom_call_target="tpu_custom_call" | custom-call | tf_op jit(solution)/shard_map/write_out/pallas_call | solution.py:305
  260.2 0.0 copy-done.1
  260.2 0.6 reduce
  260.9 0.0 copy-done
  260.9 0.6 reduce.1
Async XLA Ops:
  251.8 8.5 %copy-start.1 = (f32[1,2432]{1,0:T(1,128)S(1)}, f32[1,2432]{1,0:T(1,128)}, u32[]{:S(2)}) copy-start(f32[1,2432]{1,0:T(1,128)} %get-tuple-element.14) | copy-start | bytes 29188
  251.8 9.1 %copy-start = (f32[1,2432]{1,0:T(1,128)S(1)}, f32[1,2432]{1,0:T(1,128)}, u32[]{:S(2)}) copy-start(f32[1,2432]{1,0:T(1,128)} %get-tuple-element.15) | copy-start | bytes 29188
where the time goes:
time: 262 us
  Pallas kernels  258 us (98%)
    pallas_call x1, Pallas kernels, per_device(): pl.pallas_call(functools.partial(gather_kernel, n), out_shape=(pltpu.VMEM...  250 us
    pallas_call x1, Pallas kernels, write_out(): pl.pallas_call(functools.partial(write_kernel, pieces), out_shape=[jax.Sh...  8.43 us

commit v1 on v0

v1 whole, which is shorter than its diff:
```python
import functools

import jax
import jax.numpy as jnp
from jax import lax
from jax.experimental import pallas as pl
from jax.experimental.pallas import tpu as pltpu
from jax.sharding import PartitionSpec as P

learn_rate = 0.02
decay_rate = 0.1
tiny_value = 1e-08
lanes = 128
vmem_bytes = 67043328
block_rows = 16
MESH = pl.DeviceIdType.MESH
scope = jax.named_scope


def column_cuts(columns):
    tiles = columns // lanes
    first = max(1, tiles // 9)
    rest = tiles - first
    sizes = [first] + [rest // 3 + (1 if i < rest % 3 else 0) for i in range(3)]
    cuts, at = [], 0
    for size in sizes:
        if size:
            cuts.append((at * lanes, size * lanes))
        at += size
    return cuts


def gather_kernel(
    n, gain_ref, wg, mg, sg, wu, mu, su, out_gate, out_up, col_gate, col_up,
    held, gain_row, gain_wide, parts,
    gain_sem, in_sem, part_send, part_recv, send_sem, line_recv, mate_recv, rest_recv,
):
    me = lax.axis_index("rows")
    w = lax.axis_index("width")
    length = n // 2
    place, side = me // 2, me % 2
    mate = place + 1 - 2 * (place % 2)
    rows, columns = wg.shape
    cuts = column_cuts(columns)
    half = len(cuts)
    chunks = [(t, at, size) for t in range(2) for at, size in cuts]
    sources = ((wg, mg, sg), (wu, mu, su))
    outs = (out_gate, out_up)
    cols = (col_gate, col_up)

    barrier = pltpu.get_barrier_semaphore()

    def greet(i, carry):
        peer = lax.rem(me + i, n)
        pl.semaphore_signal(barrier, inc=1, device_id=(peer, w), device_id_type=MESH)
        return carry

    lax.fori_loop(1, n, greet, 0)

    def fetch(k):
        t, at, size = chunks[k]
        for i, src in enumerate(sources[t]):
            pltpu.make_async_copy(
                src.at[:, pl.ds(at, size)], held.at[i, t, :, pl.ds(at, size)], in_sem.at[k]
            ).start()

    def fetched(k):
        t, at, size = chunks[k]
        here = held.at[:, t, :, pl.ds(at, size)]
        pltpu.make_async_copy(here, here, in_sem.at[k]).wait()

    gain_copy = pltpu.make_async_copy(gain_ref, gain_row.at[0], gain_sem)
    gain_copy.start()
    fetch(0)
    fetch(1)
    with scope("gain"):
        gain_copy.wait()
    for r in range(0, rows, 8):
        at = r // lanes * lanes
        wide = min(lanes, rows - at)
        row = jnp.broadcast_to(gain_row[:, pl.ds(at, wide)], (8, wide))
        lane = lax.broadcasted_iota(jnp.int32, (8, wide), 1)
        here = lax.broadcasted_iota(jnp.int32, (8, wide), 0) + (r - at)
        picked = jnp.sum(jnp.where(lane == here, row, 0.0), axis=1, keepdims=True)
        gain_wide[pl.ds(r, 8), :] = jnp.broadcast_to(picked, (8, lanes))

    def part_copy(k, peer):
        t, at, size = chunks[k]
        here = parts.at[me, t, :, pl.ds(at, size)]
        return pltpu.make_async_remote_copy(
            src_ref=here, dst_ref=here, send_sem=part_send, recv_sem=part_recv.at[k],
            device_id=(peer, w), device_id_type=MESH,
        )

    def compute(k):
        t, at, size = chunks[k]
        with scope(f"fetched{k}"):
            fetched(k)

        def step(b, total):
            here = pl.ds(pl.multiple_of(b * block_rows, block_rows), block_rows)
            there = pl.ds(at, size)
            weight = held[0, t, here, there]
            latest = weight - learn_rate * (
                held[1, t, here, there] / (jnp.sqrt(held[2, t, here, there]) + tiny_value) + decay_rate * weight
            )
            gain = jnp.concatenate([gain_wide[here, :]] * (size // lanes), axis=1)
            gained = latest * gain
            held[0, t, here, there] = gained
            squared = gained * gained
            for r in range(0, block_rows, 8):
                total = total + squared[r : r + 8]
            return total

        total = lax.fori_loop(0, rows // block_rows, step, jnp.zeros((8, size), jnp.float32))
        parts[me, t, :, pl.ds(at, size)] = jnp.sum(total, axis=0, keepdims=True)

    def share_parts(k):
        def send(i, carry):
            part_copy(k, lax.rem(me + i, n)).start()
            return carry

        lax.fori_loop(1, n, send, 0)

    def parts_arrived(k):
        t, at, size = chunks[k]
        refs = parts.at[pl.ds(0, n - 1), t, :, pl.ds(at, size)]
        pltpu.make_async_copy(refs, refs, part_recv.at[k]).wait()

    def block(share, k):
        t, at, size = chunks[k]
        start = pl.multiple_of(share * rows, rows)
        return outs[t].at[pl.ds(start, rows), pl.ds(at, size)]

    def push(link, share, k, recv):
        there = ((place - 1) * 2 + side, (place + 1) * 2 + side, place * 2 + 1 - side)[link]
        here = block(share, k)
        pltpu.make_async_remote_copy(
            src_ref=here, dst_ref=here, send_sem=send_sem.at[link, chunks[k][0]], recv_sem=recv,
            device_id=(there, w), device_id_type=MESH,
        ).start()

    def arrived(share, k, recv):
        here = block(share, k)
        pltpu.make_async_copy(here, here, recv).wait()

    def push_line(link, q, k):
        push(link, q * 2 + side, k, line_recv.at[q, k])

    def push_side(q, k, own=False):
        share = q * 2 + side
        if k < half:
            push(2, share, k, rest_recv.at[0])
        elif own:
            push(2, share, k, mate_recv.at[k - half])
        else:
            @pl.when(q != mate)
            def _():
                push(2, share, k, rest_recv.at[1])

    def finish(k):
        t, at, size = chunks[k]
        with scope(f"parts{k}"):
            parts_arrived(k)
        total = parts[0, t, :, pl.ds(at, size)]
        for i in range(1, n):
            total = total + parts[i, t, :, pl.ds(at, size)]
        scale = jnp.sqrt(total)
        cols[t][:, pl.ds(at, size)] = scale

        def step(b, carry):
            here = pl.ds(pl.multiple_of(b * block_rows, block_rows), block_rows)
            there = pl.ds(pl.multiple_of(me * rows + b * block_rows, block_rows), block_rows)
            outs[t][there, pl.ds(at, size)] = (held[0, t, here, pl.ds(at, size)] / scale).astype(jnp.bfloat16)
            return carry

        lax.fori_loop(0, rows // block_rows, step, 0)

    def send_own(k):
        @pl.when(place > 0)
        def _():
            push_line(0, place, k)

        @pl.when(place < length - 1)
        def _():
            push_line(1, place, k)

        push_side(place, k, own=True)

    for k in range(2, len(chunks)):
        fetch(k)
    compute(0)
    with scope("barrier"):
        pl.semaphore_wait(barrier, n - 1)
    share_parts(0)
    for k in range(len(chunks)):
        if k + 1 < len(chunks):
            compute(k + 1)
            share_parts(k + 1)
        finish(k)
        with scope(f"own{k}"):
            send_own(k)

    def spread(d, carry):
        for k in range(len(chunks)):
            @pl.when(place + d < length)
            def _():
                q = place + d
                with scope(f"R{k}"):
                    arrived(q * 2 + side, k, line_recv.at[q, k])

                @pl.when(place > 0)
                def _():
                    push_line(0, q, k)

                push_side(q, k)

            @pl.when(place - d >= 0)
            def _():
                q = place - d
                with scope(f"L{k}"):
                    arrived(q * 2 + side, k, line_recv.at[q, k])

                @pl.when(place < length - 1)
                def _():
                    push_line(1, q, k)

                push_side(q, k)

        return carry

    middle = max(1, length // 2) + 1
    lax.fori_loop(1, middle, spread, 0)

    other = place * 2 + 1 - side
    for k in range(half, len(chunks)):
        with scope(f"X{k}"):
            arrived(other, k, mate_recv.at[k - half])

        @pl.when(mate < place)
        def _():
            push(0, other, k, rest_recv.at[2])

        @pl.when(mate > place)
        def _():
            push(1, other, k, rest_recv.at[2])

    lax.fori_loop(middle, length, spread, 0)

    def pass_bytes(t, shares, sem):
        here = outs[t].at[pl.ds(0, shares * rows)]
        pltpu.make_async_copy(here, here, sem).wait()

    with scope("rest"):
        pass_bytes(0, length, rest_recv.at[0])
        if length > 2:
            pass_bytes(1, length - 2, rest_recv.at[1])
        pass_bytes(1, 1, rest_recv.at[2])

    with scope("drain"):
        everyone = parts.at[pl.ds(0, n - 1)]
        pltpu.make_async_copy(everyone, everyone, part_send).wait()
        pass_bytes(0, length, send_sem.at[2, 0])
        pass_bytes(1, length - 1, send_sem.at[2, 1])
        for p in range(length):
            @pl.when(place == p)
            def _():
                if p > 0:
                    pass_bytes(0, length - p, send_sem.at[0, 0])
                    pass_bytes(1, length - p + p % 2, send_sem.at[0, 1])
                if p < length - 1:
                    pass_bytes(0, p + 1, send_sem.at[1, 0])
                    pass_bytes(1, p + 1 + 1 - p % 2, send_sem.at[1, 1])


def write_kernel(pieces, gate, up, col_gate, col_up, out_gate, out_up, out_col_gate, out_col_up, sem):
    step = gate.shape[0] // pieces
    for i in range(pieces):
        for t, (src, dst) in enumerate(((gate, out_gate), (up, out_up))):
            pltpu.make_async_copy(src.at[pl.ds(i * step, step)], dst.at[pl.ds(i * step, step)], sem.at[t]).start()
    small = [
        pltpu.make_async_copy(src.at[0], dst, sem.at[2 + t])
        for t, (src, dst) in enumerate(((col_gate, out_col_gate), (col_up, out_col_up)))
    ]
    for copy in small:
        copy.start()
    for t, (src, dst) in enumerate(((gate, out_gate), (up, out_up))):
        pltpu.make_async_copy(src, dst, sem.at[t]).wait()
    for copy in small:
        copy.wait()


def write_out(pieces, gate, up, col_gate, col_up):
    vmem = pl.BlockSpec(memory_space=pltpu.VMEM)
    hbm = pl.BlockSpec(memory_space=pltpu.HBM)
    flat = jax.ShapeDtypeStruct((col_gate.shape[1],), col_gate.dtype)
    return pl.pallas_call(
        functools.partial(write_kernel, pieces),
        out_shape=[jax.ShapeDtypeStruct(a.shape, a.dtype) for a in (gate, up)] + [flat, flat],
        in_specs=[vmem] * 4,
        out_specs=[hbm] * 4,
        scratch_shapes=[pltpu.SemaphoreType.DMA((4,))],
        compiler_params=pltpu.CompilerParams(vmem_limit_bytes=2**20),
        name="write_out",
    )(gate, up, col_gate, col_up)


def per_device(n, weight_gate, moment_gate, square_gate, weight_up, moment_up, square_up, norm_gain):
    rows, columns = weight_gate.shape
    half = len(column_cuts(columns))
    count = 2 * half
    vmem = pl.BlockSpec(memory_space=pltpu.VMEM)
    hbm = pl.BlockSpec(memory_space=pltpu.HBM)
    room = vmem_bytes - 2 * n * rows * columns * 2 - 3 * 2**19
    ready_gate, ready_up, column_gate, column_up = pl.pallas_call(
        functools.partial(gather_kernel, n),
        out_shape=(
            pltpu.VMEM((n * rows, columns), jnp.bfloat16),
            pltpu.VMEM((n * rows, columns), jnp.bfloat16),
            pltpu.VMEM((1, columns), jnp.float32),
            pltpu.VMEM((1, columns), jnp.float32),
        ),
        in_specs=[hbm] * 7,
        out_specs=(vmem, vmem, vmem, vmem),
        scratch_shapes=[
            pltpu.VMEM((3, 2, rows, columns), jnp.float32),
            pltpu.VMEM((1, rows), jnp.float32),
            pltpu.VMEM((rows, lanes), jnp.float32),
            pltpu.VMEM((n, 2, 1, columns), jnp.float32),
            pltpu.SemaphoreType.DMA,
            pltpu.SemaphoreType.DMA((count,)),
            pltpu.SemaphoreType.DMA,
            pltpu.SemaphoreType.DMA((count,)),
            pltpu.SemaphoreType.DMA((3, 2)),
            pltpu.SemaphoreType.DMA((n // 2, count)),
            pltpu.SemaphoreType.DMA((half,)),
            pltpu.SemaphoreType.DMA((3,)),
        ],
        compiler_params=pltpu.CompilerParams(
            collective_id=0, has_side_effects=True, vmem_limit_bytes=room
        ),
        name="step_and_gather",
    )(norm_gain, weight_gate, moment_gate, square_gate, weight_up, moment_up, square_up)
    return write_out(n, ready_gate, ready_up, column_gate, column_up)


def solution(mesh):
    split = P("rows", "width")
    return jax.shard_map(
        functools.partial(per_device, mesh.shape["rows"]),
        mesh=mesh,
        in_specs=(split,) * 6 + (P("rows"),),
        out_specs=(P(None, "width"), P(None, "width"), P("width"), P("width")),
        check_vma=False,
    )
```

time: 262 us -> 256 us (0.977)
  Pallas kernels: 258 us -> 255 us
    pallas_call x1, Pallas kernels: 250 us -> 247 us  [per_device(): pl.pallas_call(functools.partial(gather_kernel, n), out_shape=(pltpu.VMEM...]
where the time goes in v1:
time: 256 us
  Pallas kernels  255 us (100%)
    pallas_call x1, Pallas kernels, per_device(): pl.pallas_call(functools.partial(gather_kernel, n), out_shape=(pltpu.VMEM...  247 us
    pallas_call x1, Pallas kernels, write_out(): pl.pallas_call(functools.partial(write_kernel, pieces), out_shape=[jax.Sh...  8.33 us

profile of v1, /device:TPU:0, one launch (start us, length us, event | category | flops | bytes accessed | tf_op | source)
XLA Modules:
  0.0 255.6 jit_solution(2482513883390542240)
XLA Ops:
  0.6 246.7 %step_and_gather.1 = (bf16[2560,2432]{1,0:T(8,128)(2,1)S(1)}, bf16[2560,2432]{1,0:T(8,128)(2,1)S(1)}, f32[1,2432]{1,0:T(1,128)S(1)}, f32[1,2432]{1,0:T(1,128)S(1)}) custom-call(f32[320]{0:T(512)} %gain_ref.1, f32[320,2432]{1,0:T(8,128)} %wg.1, f32[320,2432]{1,0:T(8,128)} %mg.1, f32[320,2432]{1,0:T(8,128)} %sg.1, f32[320,2432]{1,0:T(8,128)} %wu.1, ...), custom_call_target="tpu_custom_call" | custom-call | tf_op jit(solution)/shard_map/step_and_gather/pallas_call | solution.py:315
  247.3 8.3 %write_out.1 = (bf16[2560,2432]{1,0:T(8,128)(2,1)}, bf16[2560,2432]{1,0:T(8,128)(2,1)}, f32[2432]{0:T(1024)}, f32[2432]{0:T(1024)}) custom-call(bf16[2560,2432]{1,0:T(8,128)(2,1)S(1)} %get-tuple-element.8.gate, bf16[2560,2432]{1,0:T(8,128)(2,1)S(1)} %get-tuple-element.9.up, f32[1,2432]{1,0:T(1,128)S(1)} %get-tuple-element.10.col_gate, ...), custom_call_target="tpu_custom_call" | custom-call | tf_op jit(solution)/shard_map/write_out/pallas_call | solution.py:297

commit v2 on v1

--- a/solution.py
+++ b/solution.py
@@ -17,33 +17,39 @@
 scope = jax.named_scope
 
 
-def column_cuts(columns):
+def column_chunks(columns):
     tiles = columns // lanes
-    first = max(1, tiles // 9)
-    rest = tiles - first
-    sizes = [first] + [rest // 3 + (1 if i < rest % 3 else 0) for i in range(3)]
-    cuts, at = [], 0
-    for size in sizes:
-        if size:
-            cuts.append((at * lanes, size * lanes))
-        at += size
-    return cuts
+    first, last = max(1, tiles // 9), max(1, (tiles + 1) // 4)
+    chunks = []
+    for t, sizes in enumerate(([first] + thirds(tiles - first), thirds(tiles - last) + [last])):
+        at = 0
+        for size in sizes:
+            if size:
+                chunks.append((t, at * lanes, size * lanes))
+            at += size
+    return chunks
+
+
+def thirds(tiles):
+    return [tiles // 3 + (1 if i < tiles % 3 else 0) for i in range(3)]
 
 
 def gather_kernel(
-    n, gain_ref, wg, mg, sg, wu, mu, su, out_gate, out_up, col_gate, col_up,
+    n, gain_ref, wg, mg, sg, wu, mu, su, out_gate, out_up, col_gate, col_up, tail_line, tail_side,
     held, gain_row, gain_wide, parts,
-    gain_sem, in_sem, part_send, part_recv, send_sem, line_recv, mate_recv, rest_recv,
+    gain_sem, in_sem, part_send, part_recv, send_sem, line_recv, mate_recv, rest_recv, tail_sem,
 ):
     me = lax.axis_index("rows")
     w = lax.axis_index("width")
     length = n // 2
     place, side = me // 2, me % 2
     mate = place + 1 - 2 * (place % 2)
+    far = jnp.where(place * 2 < length, length - 1, 0)
     rows, columns = wg.shape
-    cuts = column_cuts(columns)
-    half = len(cuts)
-    chunks = [(t, at, size) for t in range(2) for at, size in cuts]
+    chunks = column_chunks(columns)
+    half = sum(t == 0 for t, _, _ in chunks)
+    last = len(chunks) - 1
+    body = chunks[last][1]
     sources = ((wg, mg, sg), (wu, mu, su))
     outs = (out_gate, out_up)
     cols = (col_gate, col_up)
@@ -132,11 +138,11 @@
         start = pl.multiple_of(share * rows, rows)
         return outs[t].at[pl.ds(start, rows), pl.ds(at, size)]
 
-    def push(link, share, k, recv):
+    def push(link, share, k, recv, send):
         there = ((place - 1) * 2 + side, (place + 1) * 2 + side, place * 2 + 1 - side)[link]
         here = block(share, k)
         pltpu.make_async_remote_copy(
-            src_ref=here, dst_ref=here, send_sem=send_sem.at[link, chunks[k][0]], recv_sem=recv,
+            src_ref=here, dst_ref=here, send_sem=send_sem.at[send], recv_sem=recv,
             device_id=(there, w), device_id_type=MESH,
         ).start()
 
@@ -145,18 +151,22 @@
         pltpu.make_async_copy(here, here, recv).wait()
 
     def push_line(link, q, k):
-        push(link, q * 2 + side, k, line_recv.at[q, k])
+        push(link, q * 2 + side, k, line_recv.at[q, k], link * 2 + chunks[k][0])
 
     def push_side(q, k, own=False):
         share = q * 2 + side
         if k < half:
-            push(2, share, k, rest_recv.at[0])
+            push(2, share, k, rest_recv.at[0], 4)
         elif own:
-            push(2, share, k, mate_recv.at[k - half])
+            push(2, share, k, mate_recv.at[k - half], 6 if k == last else 5)
+        elif k < last:
+            @pl.when(q != mate)
+            def _():
+                push(2, share, k, rest_recv.at[1], 5)
         else:
-            @pl.when(q != mate)
-            def _():
-                push(2, share, k, rest_recv.at[1])
+            @pl.when((q != mate) & (q != far))
+            def _():
+                push(2, share, k, rest_recv.at[3], 6)
 
     def finish(k):
         t, at, size = chunks[k]
@@ -236,41 +246,48 @@
     for k in range(half, len(chunks)):
         with scope(f"X{k}"):
             arrived(other, k, mate_recv.at[k - half])
-
-        @pl.when(mate < place)
-        def _():
-            push(0, other, k, rest_recv.at[2])
-
-        @pl.when(mate > place)
-        def _():
-            push(1, other, k, rest_recv.at[2])
-
+        if k < last:
+            @pl.when(mate < place)
+            def _():
+                push(0, other, k, rest_recv.at[2], 7)
+
+            @pl.when(mate > place)
+            def _():
+                push(1, other, k, rest_recv.at[2], 7)
+
+    line_copy = pltpu.make_async_copy(block(other, last), tail_line, tail_sem.at[0])
+    line_copy.start()
     lax.fori_loop(middle, length, spread, 0)
-
-    def pass_bytes(t, shares, sem):
-        here = outs[t].at[pl.ds(0, shares * rows)]
+    side_copy = pltpu.make_async_copy(block(far * 2 + side, last), tail_side, tail_sem.at[1])
+    side_copy.start()
+
+    def pass_bytes(t, shares, sem, at=0, size=columns):
+        here = outs[t].at[pl.ds(0, shares * rows), pl.ds(at, size)]
         pltpu.make_async_copy(here, here, sem).wait()
 
     with scope("rest"):
         pass_bytes(0, length, rest_recv.at[0])
-        if length > 2:
-            pass_bytes(1, length - 2, rest_recv.at[1])
-        pass_bytes(1, 1, rest_recv.at[2])
+        pass_bytes(1, length - 2, rest_recv.at[1], 0, body)
+        pass_bytes(1, 1, rest_recv.at[2], 0, body)
+        pass_bytes(1, length - 3, rest_recv.at[3], body, columns - body)
 
     with scope("drain"):
         everyone = parts.at[pl.ds(0, n - 1)]
         pltpu.make_async_copy(everyone, everyone, part_send).wait()
-        pass_bytes(0, length, send_sem.at[2, 0])
-        pass_bytes(1, length - 1, send_sem.at[2, 1])
+        pass_bytes(0, length, send_sem.at[4])
+        pass_bytes(1, length - 1, send_sem.at[5], 0, body)
+        pass_bytes(1, length - 2, send_sem.at[6], body, columns - body)
+        pass_bytes(1, 1, send_sem.at[7], 0, body)
         for p in range(length):
             @pl.when(place == p)
             def _():
-                if p > 0:
-                    pass_bytes(0, length - p, send_sem.at[0, 0])
-                    pass_bytes(1, length - p + p % 2, send_sem.at[0, 1])
-                if p < length - 1:
-                    pass_bytes(0, p + 1, send_sem.at[1, 0])
-                    pass_bytes(1, p + 1 + 1 - p % 2, send_sem.at[1, 1])
+                for t in range(2):
+                    if p > 0:
+                        pass_bytes(t, length - p, send_sem.at[t])
+                    if p < length - 1:
+                        pass_bytes(t, p + 1, send_sem.at[2 + t])
+        line_copy.wait()
+        side_copy.wait()
 
 
 def write_kernel(pieces, gate, up, col_gate, col_up, out_gate, out_up, out_col_gate, out_col_up, sem):
@@ -301,27 +318,64 @@
         out_specs=[hbm] * 4,
         scratch_shapes=[pltpu.SemaphoreType.DMA((4,))],
         compiler_params=pltpu.CompilerParams(vmem_limit_bytes=2**20),
+        cost_estimate=pl.CostEstimate(flops=10**8, bytes_accessed=4 * gate.size, transcendentals=0),
         name="write_out",
     )(gate, up, col_gate, col_up)
 
 
+def place_kernel(n, up, from_line, from_side, out, sem):
+    me = lax.axis_index("rows")
+    place, side = me // 2, me % 2
+    mate = place + 1 - 2 * (place % 2)
+    far = jnp.where(place * 2 < n // 2, n // 2 - 1, 0)
+    rows, tail = from_line.shape
+    copies = []
+    for i, (src, q) in enumerate(((from_line, mate), (from_side, far))):
+        start = pl.multiple_of((q * 2 + 1 - side) * rows, rows)
+        there = out.at[pl.ds(start, rows), pl.ds(out.shape[1] - tail, tail)]
+        copies.append(pltpu.make_async_copy(src, there, sem.at[i]))
+    for copy in copies:
+        copy.start()
+    for copy in copies:
+        copy.wait()
+
+
+def place_tails(n, up, from_line, from_side):
+    vmem = pl.BlockSpec(memory_space=pltpu.VMEM)
+    hbm = pl.BlockSpec(memory_space=pltpu.HBM)
+    return pl.pallas_call(
+        functools.partial(place_kernel, n),
+        out_shape=jax.ShapeDtypeStruct(up.shape, up.dtype),
+        in_specs=[hbm, vmem, vmem],
+        out_specs=hbm,
+        input_output_aliases={0: 0},
+        scratch_shapes=[pltpu.SemaphoreType.DMA((2,))],
+        compiler_params=pltpu.CompilerParams(vmem_limit_bytes=2**20),
+        name="place_tails",
+    )(up, from_line, from_side)
+
+
 def per_device(n, weight_gate, moment_gate, square_gate, weight_up, moment_up, square_up, norm_gain):
     rows, columns = weight_gate.shape
-    half = len(column_cuts(columns))
-    count = 2 * half
+    length = n // 2
+    chunks = column_chunks(columns)
+    count, tail = len(chunks), chunks[-1][2]
+    up_count = sum(t for t, _, _ in chunks)
     vmem = pl.BlockSpec(memory_space=pltpu.VMEM)
     hbm = pl.BlockSpec(memory_space=pltpu.HBM)
     room = vmem_bytes - 2 * n * rows * columns * 2 - 3 * 2**19
-    ready_gate, ready_up, column_gate, column_up = pl.pallas_call(
+    ready_gate, ready_up, column_gate, column_up, tail_line, tail_side = pl.pallas_call(
         functools.partial(gather_kernel, n),
         out_shape=(
             pltpu.VMEM((n * rows, columns), jnp.bfloat16),
             pltpu.VMEM((n * rows, columns), jnp.bfloat16),
             pltpu.VMEM((1, columns), jnp.float32),
             pltpu.VMEM((1, columns), jnp.float32),
+            jax.ShapeDtypeStruct((rows, tail), jnp.bfloat16),
+            jax.ShapeDtypeStruct((rows, tail), jnp.bfloat16),
         ),
         in_specs=[hbm] * 7,
-        out_specs=(vmem, vmem, vmem, vmem),
+        out_specs=(vmem, vmem, vmem, vmem, hbm, hbm),
         scratch_shapes=[
             pltpu.VMEM((3, 2, rows, columns), jnp.float32),
             pltpu.VMEM((1, rows), jnp.float32),
@@ -331,17 +385,24 @@
             pltpu.SemaphoreType.DMA((count,)),
             pltpu.SemaphoreType.DMA,
             pltpu.SemaphoreType.DMA((count,)),
-            pltpu.SemaphoreType.DMA((3, 2)),
-            pltpu.SemaphoreType.DMA((n // 2, count)),
-            pltpu.SemaphoreType.DMA((half,)),
-            pltpu.SemaphoreType.DMA((3,)),
+            pltpu.SemaphoreType.DMA((8,)),
+            pltpu.SemaphoreType.DMA((length, count)),
+            pltpu.SemaphoreType.DMA((up_count,)),
+            pltpu.SemaphoreType.DMA((4,)),
+            pltpu.SemaphoreType.DMA((2,)),
         ],
         compiler_params=pltpu.CompilerParams(
             collective_id=0, has_side_effects=True, vmem_limit_bytes=room
         ),
         name="step_and_gather",
     )(norm_gain, weight_gate, moment_gate, square_gate, weight_up, moment_up, square_up)
-    return write_out(n, ready_gate, ready_up, column_gate, column_up)
+    swap_line = [(i, (i // 2 ^ 1) * 2 + i % 2) for i in range(n)]
+    swap_side = [(i, i ^ 1) for i in range(n)]
+    from_line = lax.ppermute(tail_line, "rows", swap_line)
+    from_side = lax.ppermute(tail_side, "rows", swap_side)
+    ready_gate, ready_up, column_gate, column_up = write_out(n, ready_gate, ready_up, column_gate, column_up)
+    ready_up = place_tails(n, ready_up, from_line, from_side)
+    return ready_gate, ready_up, column_gate, column_up
 
 
 def solution(mesh):

time: 256 us -> 250 us (0.977)
  Pallas kernels: 255 us -> 247 us
    pallas_call x1, Pallas kernels: 247 us -> 238 us  [per_device(): pl.pallas_call(functools.partial(gather_kernel, n), out_shape=(pltpu.VMEM...]
  transfers between devices with their start and end apart: 0 -> 2, of which waited for: 0 -> 2; matrix products, arithmetic and copies ran while one was open for 0% -> 0% of each run, Pallas kernels for 0% -> 3%
where the time goes in v2:
time: 250 us
  Pallas kernels  247 us (99%)
    pallas_call x1, Pallas kernels, per_device(): pl.pallas_call(functools.partial(gather_kernel, n), out_shape=(pltpu.VMEM...  238 us
    pallas_call x1, Pallas kernels, write_out(): pl.pallas_call(functools.partial(write_kernel, pieces), out_shape=[jax.Sh...  8.32 us
  transfers between devices with their start and end apart: 2, of which 2 were waited for; matrix products, arithmetic and copies ran while one was open for 0% of the time, Pallas kernels for 3%

profile of v2, /device:TPU:0, one launch (start us, length us, event | category | flops | bytes accessed | tf_op | source)
XLA Modules:
  0.0 249.6 jit_solution(15977936416379100237)
XLA Ops:
  0.6 237.9 %step_and_gather.1 = (bf16[2560,2432]{1,0:T(8,128)(2,1)S(1)}, bf16[2560,2432]{1,0:T(8,128)(2,1)S(1)}, f32[1,2432]{1,0:T(1,128)S(1)}, f32[1,2432]{1,0:T(1,128)S(1...) custom-call(f32[320]{0:T(512)} %gain_ref.1, f32[320,2432]{1,0:T(8,128)} %wg.1, f32[320,2432]{1,0:T(8,128)} %mg.1, ...), custom_call_target="tpu_custom_call" | custom-call | tf_op jit(solution)/shard_map/step_and_gather/pallas_call | solution.py:367
  238.6 0.1 collective-permute-start
  238.7 1.4 collective-permute-start.1
  240.0 8.3 %write_out.1 = (bf16[2560,2432]{1,0:T(8,128)(2,1)}, bf16[2560,2432]{1,0:T(8,128)(2,1)}, f32[2432]{0:T(1024)}, f32[2432]{0:T(1024)}) custom-call(bf16[2560,2432]{1,0:T(8,128)(2,1)S(1)} %get-tuple-element.14.gate, bf16[2560,2432]{1,0:T(8,128)(2,1)S(1)} %get-tuple-element.15.up, f32[1,2432]{1,0:T(1,128)S(1)} %get-tuple-element.16.col_gate, ...), custom_call_target="tpu_custom_call" | custom-call | flops 100000000 | bytes 24903680 | tf_op jit(solution)/shard_map/write_out/pallas_call | solution.py:314
  248.4 0.2 collective-permute-done.from_line
  248.6 0.1 collective-permute-done.1.from_side
  248.7 0.9 place_tails.1
Async XLA Ops:
  238.6 10.0 %collective-permute-start = (bf16[320,640]{1,0:T(8,128)(2,1)}, bf16[320,640]{1,0:T(8,128)(2,1)S(1)}, u32[]{:S(2)}, u32[]{:S(2)}) collective-permute-start(bf16[320,640]{1,0:T(8,128)(2,1)} %get-tuple-element.20), channel_id=1, source_target_pairs={{0,8},{4,12},{8,0},{12,4},{16,24},{20,28},{24,16},{28,20},{1,9},{5... | collective-permute-start | bytes 1228808 | tf_op jit(solution)/shard_map/ppermute | solution.py:401
  238.7 10.0 %collective-permute-start.1 = (bf16[320,640]{1,0:T(8,128)(2,1)}, bf16[320,640]{1,0:T(8,128)(2,1)S(1)}, u32[]{:S(2)}, u32[]{:S(2)}) collective-permute-start(bf16[320,640]{1,0:T(8,128)(2,1)} %get-tuple-element.21), channel_id=1, source_target_pairs={{0,4},{4,0},{8,12},{12,8},{16,20},{20,16},{24,28},{28,24},{1,5},{5... | collective-permute-start | bytes 1228808 | tf_op jit(solution)/shard_map/ppermute | solution.py:402

commit v3 on v2

--- a/solution.py
+++ b/solution.py
@@ -19,37 +19,39 @@
 
 def column_chunks(columns):
     tiles = columns // lanes
-    first, last = max(1, tiles // 9), max(1, (tiles + 1) // 4)
+    first, second, last = max(1, tiles // 9), max(1, (tiles + 1) // 4), max(1, tiles * 3 // 8)
+    gate = [first, second] + even(tiles - first - second, 2)
+    up = even(tiles - last, 3) + [last]
     chunks = []
-    for t, sizes in enumerate(([first] + thirds(tiles - first), thirds(tiles - last) + [last])):
-        at = 0
+    for t, sizes, at in ((0, gate, 0), (1, up, last)):
         for size in sizes:
             if size:
-                chunks.append((t, at * lanes, size * lanes))
+                chunks.append((t, at % tiles * lanes, size * lanes))
             at += size
     return chunks
 
 
-def thirds(tiles):
-    return [tiles // 3 + (1 if i < tiles % 3 else 0) for i in range(3)]
+def even(tiles, pieces):
+    return [tiles // pieces + (1 if i < tiles % pieces else 0) for i in range(pieces)]
 
 
 def gather_kernel(
     n, gain_ref, wg, mg, sg, wu, mu, su, out_gate, out_up, col_gate, col_up, tail_line, tail_side,
-    held, gain_row, gain_wide, parts,
-    gain_sem, in_sem, part_send, part_recv, send_sem, line_recv, mate_recv, rest_recv, tail_sem,
+    held, gain_row, gain_wide, parts, raw,
+    gain_sem, in_sem, part_send, part_recv, send_sem, line_recv, mate_recv, rest_recv, tail_sem, raw_send, raw_recv,
 ):
     me = lax.axis_index("rows")
     w = lax.axis_index("width")
     length = n // 2
     place, side = me // 2, me % 2
     mate = place + 1 - 2 * (place % 2)
+    lead = w % 2 == 1
     far = jnp.where(place * 2 < length, length - 1, 0)
     rows, columns = wg.shape
     chunks = column_chunks(columns)
     half = sum(t == 0 for t, _, _ in chunks)
     last = len(chunks) - 1
-    body = chunks[last][1]
+    start, tail = chunks[0][2], chunks[last][2]
     sources = ((wg, mg, sg), (wu, mu, su))
     outs = (out_gate, out_up)
     cols = (col_gate, col_up)
@@ -90,11 +92,17 @@
         picked = jnp.sum(jnp.where(lane == here, row, 0.0), axis=1, keepdims=True)
         gain_wide[pl.ds(r, 8), :] = jnp.broadcast_to(picked, (8, lanes))
 
-    def part_copy(k, peer):
-        t, at, size = chunks[k]
+    groups = [[0, 1], list(range(2, half)), list(range(half, len(chunks)))]
+
+    def span(g):
+        t = chunks[groups[g][0]][0]
+        return t, min(chunks[k][1] for k in groups[g]), sum(chunks[k][2] for k in groups[g])
+
+    def part_copy(g, peer):
+        t, at, size = span(g)
         here = parts.at[me, t, :, pl.ds(at, size)]
         return pltpu.make_async_remote_copy(
-            src_ref=here, dst_ref=here, send_sem=part_send, recv_sem=part_recv.at[k],
+            src_ref=here, dst_ref=here, send_sem=part_send, recv_sem=part_recv.at[g],
             device_id=(peer, w), device_id_type=MESH,
         )
 
@@ -121,17 +129,17 @@
         total = lax.fori_loop(0, rows // block_rows, step, jnp.zeros((8, size), jnp.float32))
         parts[me, t, :, pl.ds(at, size)] = jnp.sum(total, axis=0, keepdims=True)
 
-    def share_parts(k):
+    def share_parts(g):
         def send(i, carry):
-            part_copy(k, lax.rem(me + i, n)).start()
+            part_copy(g, lax.rem(me + i, n)).start()
             return carry
 
         lax.fori_loop(1, n, send, 0)
 
-    def parts_arrived(k):
-        t, at, size = chunks[k]
+    def parts_arrived(g):
+        t, at, size = span(g)
         refs = parts.at[pl.ds(0, n - 1), t, :, pl.ds(at, size)]
-        pltpu.make_async_copy(refs, refs, part_recv.at[k]).wait()
+        pltpu.make_async_copy(refs, refs, part_recv.at[g]).wait()
 
     def block(share, k):
         t, at, size = chunks[k]
@@ -151,11 +159,13 @@
         pltpu.make_async_copy(here, here, recv).wait()
 
     def push_line(link, q, k):
-        push(link, q * 2 + side, k, line_recv.at[q, k], link * 2 + chunks[k][0])
+        push(link, q * 2 + side, k, line_recv.at[q, k], 8 + link if k == 0 else link * 2 + chunks[k][0])
 
     def push_side(q, k, own=False):
         share = q * 2 + side
-        if k < half:
+        if k == 0:
+            push(2, share, k, rest_recv.at[4], 10)
+        elif k < half:
             push(2, share, k, rest_recv.at[0], 4)
         elif own:
             push(2, share, k, mate_recv.at[k - half], 6 if k == last else 5)
@@ -168,10 +178,57 @@
             def _():
                 push(2, share, k, rest_recv.at[3], 6)
 
+    def raw_copy(link):
+        t, at, size = chunks[0]
+        there = ((place - 1) * 2 + side, (place + 1) * 2 + side, place * 2 + 1 - side)[link]
+        return pltpu.make_async_remote_copy(
+            src_ref=held.at[0, t, :, pl.ds(at, size)], dst_ref=raw.at[link],
+            send_sem=raw_send.at[link], recv_sem=raw_recv.at[link],
+            device_id=(there, w), device_id_type=MESH,
+        )
+
+    def each_raw(action):
+        @pl.when(place > 0)
+        def _():
+            action(raw_copy(0))
+
+        @pl.when(place < length - 1)
+        def _():
+            action(raw_copy(1))
+
+        action(raw_copy(2))
+
+    def take_raw(link, share):
+        t, at, size = chunks[0]
+        pltpu.make_async_copy(raw.at[link], raw.at[link], raw_recv.at[link]).wait()
+        scale = cols[t][:, pl.ds(at, size)]
+
+        def step(b, carry):
+            here = pl.ds(pl.multiple_of(b * block_rows, block_rows), block_rows)
+            there = pl.ds(pl.multiple_of(share * rows + b * block_rows, block_rows), block_rows)
+            outs[t][there, pl.ds(at, size)] = (raw[link, here, :] / scale).astype(jnp.bfloat16)
+            return carry
+
+        lax.fori_loop(0, rows // block_rows, step, 0)
+
+    def line_arrived(q, k, d, link):
+        if k == 0:
+            @pl.when(lead & (d == 1))
+            def _():
+                take_raw(link, q * 2 + side)
+
+            @pl.when(jnp.logical_not(lead & (d == 1)))
+            def _():
+                arrived(q * 2 + side, k, line_recv.at[q, k])
+        else:
+            arrived(q * 2 + side, k, line_recv.at[q, k])
+
     def finish(k):
         t, at, size = chunks[k]
-        with scope(f"parts{k}"):
-            parts_arrived(k)
+        for g, group in enumerate(groups):
+            if k == (1 if g == 0 else group[0]):
+                with scope(f"parts{g}"):
+                    parts_arrived(g)
         total = parts[0, t, :, pl.ds(at, size)]
         for i in range(1, n):
             total = total + parts[i, t, :, pl.ds(at, size)]
@@ -200,16 +257,36 @@
     for k in range(2, len(chunks)):
         fetch(k)
     compute(0)
+    compute(1)
     with scope("barrier"):
         pl.semaphore_wait(barrier, n - 1)
-    share_parts(0)
-    for k in range(len(chunks)):
-        if k + 1 < len(chunks):
-            compute(k + 1)
-            share_parts(k + 1)
+
+    @pl.when(lead)
+    def _():
+        share_parts(0)
+        each_raw(lambda copy: copy.start())
+
+    for k in groups[1]:
+        compute(k)
+
+    @pl.when(jnp.logical_not(lead))
+    def _():
+        share_parts(0)
+
+    share_parts(1)
+    for k in [1, 0] + list(range(2, len(chunks))):
         finish(k)
         with scope(f"own{k}"):
-            send_own(k)
+            if k == 0:
+                @pl.when(jnp.logical_not(lead))
+                def _():
+                    send_own(k)
+            else:
+                send_own(k)
+        if k == 0:
+            for i in groups[2]:
+                compute(i)
+            share_parts(2)
 
     def spread(d, carry):
         for k in range(len(chunks)):
@@ -217,7 +294,7 @@
             def _():
                 q = place + d
                 with scope(f"R{k}"):
-                    arrived(q * 2 + side, k, line_recv.at[q, k])
+                    line_arrived(q, k, d, 0)
 
                 @pl.when(place > 0)
                 def _():
@@ -229,7 +306,7 @@
             def _():
                 q = place - d
                 with scope(f"L{k}"):
-                    arrived(q * 2 + side, k, line_recv.at[q, k])
+                    line_arrived(q, k, d, 1)
 
                 @pl.when(place < length - 1)
                 def _():
@@ -266,26 +343,54 @@
         pltpu.make_async_copy(here, here, sem).wait()
 
     with scope("rest"):
-        pass_bytes(0, length, rest_recv.at[0])
-        pass_bytes(1, length - 2, rest_recv.at[1], 0, body)
-        pass_bytes(1, 1, rest_recv.at[2], 0, body)
-        pass_bytes(1, length - 3, rest_recv.at[3], body, columns - body)
+        pass_bytes(0, length, rest_recv.at[0], start, columns - start)
+
+        @pl.when(lead)
+        def _():
+            pass_bytes(0, length - 1, rest_recv.at[4], 0, start)
+            take_raw(2, other)
+
+        @pl.when(jnp.logical_not(lead))
+        def _():
+            pass_bytes(0, length, rest_recv.at[4], 0, start)
+
+        pass_bytes(1, length - 2, rest_recv.at[1], tail, columns - tail)
+        pass_bytes(1, 1, rest_recv.at[2], tail, columns - tail)
+        pass_bytes(1, length - 3, rest_recv.at[3], 0, tail)
 
     with scope("drain"):
         everyone = parts.at[pl.ds(0, n - 1)]
         pltpu.make_async_copy(everyone, everyone, part_send).wait()
-        pass_bytes(0, length, send_sem.at[4])
-        pass_bytes(1, length - 1, send_sem.at[5], 0, body)
-        pass_bytes(1, length - 2, send_sem.at[6], body, columns - body)
-        pass_bytes(1, 1, send_sem.at[7], 0, body)
+        pass_bytes(0, length, send_sem.at[4], start, columns - start)
+        pass_bytes(1, length - 1, send_sem.at[5], tail, columns - tail)
+        pass_bytes(1, length - 2, send_sem.at[6], 0, tail)
+        pass_bytes(1, 1, send_sem.at[7], tail, columns - tail)
         for p in range(length):
             @pl.when(place == p)
             def _():
-                for t in range(2):
-                    if p > 0:
-                        pass_bytes(t, length - p, send_sem.at[t])
-                    if p < length - 1:
-                        pass_bytes(t, p + 1, send_sem.at[2 + t])
+                for link, shares in ((0, length - p), (1, p + 1)):
+                    if (p, link) not in ((0, 0), (length - 1, 1)):
+                        pass_bytes(0, shares, send_sem.at[link * 2], start, columns - start)
+                        pass_bytes(1, shares, send_sem.at[link * 2 + 1])
+
+        def first_sent(own):
+            pass_bytes(0, length - 1 + own, send_sem.at[10], 0, start)
+            for p in range(length):
+                @pl.when(place == p)
+                def _():
+                    for link, shares in ((0, length - p - 1 + own), (1, p + own)):
+                        if shares and (p, link) not in ((0, 0), (length - 1, 1)):
+                            pass_bytes(0, shares, send_sem.at[8 + link], 0, start)
+
+        @pl.when(lead)
+        def _():
+            first_sent(0)
+            each_raw(lambda copy: copy.wait_send())
+
+        @pl.when(jnp.logical_not(lead))
+        def _():
+            first_sent(1)
+
         line_copy.wait()
         side_copy.wait()
 
@@ -332,7 +437,7 @@
     copies = []
     for i, (src, q) in enumerate(((from_line, mate), (from_side, far))):
         start = pl.multiple_of((q * 2 + 1 - side) * rows, rows)
-        there = out.at[pl.ds(start, rows), pl.ds(out.shape[1] - tail, tail)]
+        there = out.at[pl.ds(start, rows), pl.ds(0, tail)]
         copies.append(pltpu.make_async_copy(src, there, sem.at[i]))
     for copy in copies:
         copy.start()
@@ -350,7 +455,7 @@
         out_specs=hbm,
         input_output_aliases={0: 0},
         scratch_shapes=[pltpu.SemaphoreType.DMA((2,))],
-        compiler_params=pltpu.CompilerParams(vmem_limit_bytes=2**20),
+        compiler_params=pltpu.CompilerParams(vmem_limit_bytes=2**22),
         name="place_tails",
     )(up, from_line, from_side)
 
@@ -381,15 +486,18 @@
             pltpu.VMEM((1, rows), jnp.float32),
             pltpu.VMEM((rows, lanes), jnp.float32),
             pltpu.VMEM((n, 2, 1, columns), jnp.float32),
+            pltpu.VMEM((3, rows, chunks[0][2]), jnp.float32),
             pltpu.SemaphoreType.DMA,
             pltpu.SemaphoreType.DMA((count,)),
             pltpu.SemaphoreType.DMA,
-            pltpu.SemaphoreType.DMA((count,)),
-            pltpu.SemaphoreType.DMA((8,)),
+            pltpu.SemaphoreType.DMA((3,)),
+            pltpu.SemaphoreType.DMA((11,)),
             pltpu.SemaphoreType.DMA((length, count)),
             pltpu.SemaphoreType.DMA((up_count,)),
-            pltpu.SemaphoreType.DMA((4,)),
+            pltpu.SemaphoreType.DMA((5,)),
             pltpu.SemaphoreType.DMA((2,)),
+            pltpu.SemaphoreType.DMA((3,)),
+            pltpu.SemaphoreType.DMA((3,)),
         ],
         compiler_params=pltpu.CompilerParams(
             collective_id=0, has_side_effects=True, vmem_limit_bytes=room

time: 250 us -> 247 us (0.988)
  Pallas kernels: 247 us -> 244 us
    pallas_call x1, Pallas kernels: 238 us -> 235 us  [per_device(): pl.pallas_call(functools.partial(gather_kernel, n), out_shape=(pltpu.VMEM...]
  transfers between devices with their start and end apart: 2 -> 2, of which waited for: 2 -> 1; matrix products, arithmetic and copies ran while one was open for 0% -> 0% of each run, Pallas kernels for 3% -> 3%
where the time goes in v3:
time: 247 us
  Pallas kernels  244 us (99%)
    pallas_call x1, Pallas kernels, per_device(): pl.pallas_call(functools.partial(gather_kernel, n), out_shape=(pltpu.VMEM...  235 us
    pallas_call x1, Pallas kernels, write_out(): pl.pallas_call(functools.partial(write_kernel, pieces), out_shape=[jax.Sh...  8.32 us
  transfers between devices with their start and end apart: 2, of which 1 were waited for; matrix products, arithmetic and copies ran while one was open for 0% of the time, Pallas kernels for 3%

profile of v3, /device:TPU:0, one launch (start us, length us, event | category | flops | bytes accessed | tf_op | source)
XLA Modules:
  0.0 246.6 jit_solution(17326950308002205510)
XLA Ops:
  0.6 234.8 %step_and_gather.1 = (bf16[2560,2432]{1,0:T(8,128)(2,1)S(1)}, bf16[2560,2432]{1,0:T(8,128)(2,1)S(1)}, f32[1,2432]{1,0:T(1,128)S(1)}, f32[1,2432]{1,0:T(1,128)S(1...) custom-call(f32[320]{0:T(512)} %gain_ref.1, f32[320,2432]{1,0:T(8,128)} %wg.1, f32[320,2432]{1,0:T(8,128)} %mg.1, ...), custom_call_target="tpu_custom_call" | custom-call | tf_op jit(solution)/shard_map/step_and_gather/pallas_call | solution.py:472
  235.5 0.1 collective-permute-start
  235.6 0.7 collective-permute-start.1
  236.3 8.3 %write_out.1 = (bf16[2560,2432]{1,0:T(8,128)(2,1)}, bf16[2560,2432]{1,0:T(8,128)(2,1)}, f32[2432]{0:T(1024)}, f32[2432]{0:T(1024)}) custom-call(bf16[2560,2432]{1,0:T(8,128)(2,1)S(1)} %get-tuple-element.14.gate, bf16[2560,2432]{1,0:T(8,128)(2,1)S(1)} %get-tuple-element.15.up, f32[1,2432]{1,0:T(1,128)S(1)} %get-tuple-element.16.col_gate, ...), custom_call_target="tpu_custom_call" | custom-call | flops 100000000 | bytes 24903680 | tf_op jit(solution)/shard_map/write_out/pallas_call | solution.py:419
  244.6 0.9 collective-permute-done.from_line
  245.5 0.0 collective-permute-done.1.from_side
  245.6 1.0 place_tails.1
Async XLA Ops:
  235.5 10.1 %collective-permute-start = (bf16[320,896]{1,0:T(8,128)(2,1)}, bf16[320,896]{1,0:T(8,128)(2,1)S(1)}, u32[]{:S(2)}, u32[]{:S(2)}) collective-permute-start(bf16[320,896]{1,0:T(8,128)(2,1)} %get-tuple-element.20), channel_id=1, source_target_pairs={{0,8},{4,12},{8,0},{12,4},{16,24},{20,28},{24,16},{28,20},{1,9},{5... | collective-permute-start | bytes 1720328 | tf_op jit(solution)/shard_map/ppermute | solution.py:509
  235.6 10.0 %collective-permute-start.1 = (bf16[320,896]{1,0:T(8,128)(2,1)}, bf16[320,896]{1,0:T(8,128)(2,1)S(1)}, u32[]{:S(2)}, u32[]{:S(2)}) collective-permute-start(bf16[320,896]{1,0:T(8,128)(2,1)} %get-tuple-element.21), channel_id=1, source_target_pairs={{0,4},{4,0},{8,12},{12,8},{16,20},{20,16},{24,28},{28,24},{1,5},{5... | collective-permute-start | bytes 1720328 | tf_op jit(solution)/shard_map/ppermute | solution.py:510

commit v4 on v3

--- a/solution.py
+++ b/solution.py
@@ -19,7 +19,7 @@
 
 def column_chunks(columns):
     tiles = columns // lanes
-    first, second, last = max(1, tiles // 9), max(1, (tiles + 1) // 4), max(1, tiles * 3 // 8)
+    first, second, last = max(1, tiles // 9), max(1, tiles // 4), max(1, tiles * 3 // 8)
     gate = [first, second] + even(tiles - first - second, 2)
     up = even(tiles - last, 3) + [last]
     chunks = []
@@ -37,8 +37,8 @@
 
 def gather_kernel(
     n, gain_ref, wg, mg, sg, wu, mu, su, out_gate, out_up, col_gate, col_up, tail_line, tail_side,
-    held, gain_row, gain_wide, parts, raw,
-    gain_sem, in_sem, part_send, part_recv, send_sem, line_recv, mate_recv, rest_recv, tail_sem, raw_send, raw_recv,
+    held, gain_row, gain_wide, parts, pairs, raw,
+    gain_sem, in_sem, part_send, part_recv, pair_recv, send_sem, line_recv, mate_recv, rest_recv, tail_sem, raw_send, raw_recv,
 ):
     me = lax.axis_index("rows")
     w = lax.axis_index("width")
@@ -98,11 +98,11 @@
         t = chunks[groups[g][0]][0]
         return t, min(chunks[k][1] for k in groups[g]), sum(chunks[k][2] for k in groups[g])
 
-    def part_copy(g, peer):
+    def part_copy(g, source, slot, peer, recv):
         t, at, size = span(g)
-        here = parts.at[me, t, :, pl.ds(at, size)]
+        here = source.at[slot, t, :, pl.ds(at, size)]
         return pltpu.make_async_remote_copy(
-            src_ref=here, dst_ref=here, send_sem=part_send, recv_sem=part_recv.at[g],
+            src_ref=here, dst_ref=here, send_sem=part_send.at[t], recv_sem=recv.at[g],
             device_id=(peer, w), device_id_type=MESH,
         )
 
@@ -131,15 +131,48 @@
 
     def share_parts(g):
         def send(i, carry):
-            part_copy(g, lax.rem(me + i, n)).start()
+            part_copy(g, parts, me, lax.rem(me + i, n), part_recv).start()
             return carry
 
         lax.fori_loop(1, n, send, 0)
 
+    def share_pair(g):
+        part_copy(g, parts, me, place * 2 + 1 - side, pair_recv).start()
+
+    def share_line(g):
+        t, at, size = span(g)
+        there = pl.ds(at, size)
+        one = parts.at[0, t, :, there]
+        pltpu.make_async_copy(one, one, pair_recv.at[g]).wait()
+        pairs[place, t, :, there] = parts[me, t, :, there] + parts[place * 2 + 1 - side, t, :, there]
+
+        def send(i, carry):
+            part_copy(g, pairs, place, lax.rem(place + i, length) * 2 + side, part_recv).start()
+            return carry
+
+        lax.fori_loop(1, length, send, 0)
+
+    def gather_parts(g, source, count):
+        t, at, size = span(g)
+        there = pl.ds(at, size)
+        refs = source.at[pl.ds(0, count - 1), t, :, there]
+        pltpu.make_async_copy(refs, refs, part_recv.at[g]).wait()
+        total = source[0, t, :, there]
+        for i in range(1, count):
+            total = total + source[i, t, :, there]
+        cols[t][:, there] = jnp.sqrt(total)
+
     def parts_arrived(g):
-        t, at, size = span(g)
-        refs = parts.at[pl.ds(0, n - 1), t, :, pl.ds(at, size)]
-        pltpu.make_async_copy(refs, refs, part_recv.at[g]).wait()
+        if g == 2:
+            gather_parts(g, pairs, length)
+        else:
+            @pl.when(lead)
+            def _():
+                gather_parts(g, parts, n)
+
+            @pl.when(jnp.logical_not(lead))
+            def _():
+                gather_parts(g, pairs, length)
 
     def block(share, k):
         t, at, size = chunks[k]
@@ -229,11 +262,7 @@
             if k == (1 if g == 0 else group[0]):
                 with scope(f"parts{g}"):
                     parts_arrived(g)
-        total = parts[0, t, :, pl.ds(at, size)]
-        for i in range(1, n):
-            total = total + parts[i, t, :, pl.ds(at, size)]
-        scale = jnp.sqrt(total)
-        cols[t][:, pl.ds(at, size)] = scale
+        scale = cols[t][:, pl.ds(at, size)]
 
         def step(b, carry):
             here = pl.ds(pl.multiple_of(b * block_rows, block_rows), block_rows)
@@ -266,15 +295,31 @@
         share_parts(0)
         each_raw(lambda copy: copy.start())
 
+    @pl.when(jnp.logical_not(lead))
+    def _():
+        share_pair(0)
+
     for k in groups[1]:
         compute(k)
 
+    @pl.when(lead)
+    def _():
+        share_parts(1)
+
     @pl.when(jnp.logical_not(lead))
     def _():
-        share_parts(0)
-
-    share_parts(1)
+        share_pair(1)
+        with scope("line"):
+            share_line(0)
+        for i in groups[2]:
+            compute(i)
+        share_pair(2)
+        share_line(1)
+
     for k in [1, 0] + list(range(2, len(chunks))):
+        if k == groups[1][-1]:
+            with scope("line2"):
+                share_line(2)
         finish(k)
         with scope(f"own{k}"):
             if k == 0:
@@ -284,9 +329,11 @@
             else:
                 send_own(k)
         if k == 0:
-            for i in groups[2]:
-                compute(i)
-            share_parts(2)
+            @pl.when(lead)
+            def _():
+                for i in groups[2]:
+                    compute(i)
+                share_pair(2)
 
     def spread(d, carry):
         for k in range(len(chunks)):
@@ -359,8 +406,20 @@
         pass_bytes(1, length - 3, rest_recv.at[3], 0, tail)
 
     with scope("drain"):
-        everyone = parts.at[pl.ds(0, n - 1)]
-        pltpu.make_async_copy(everyone, everyone, part_send).wait()
+        def parts_sent(t, count):
+            sent = parts.at[pl.ds(0, count), t]
+            pltpu.make_async_copy(sent, sent, part_send.at[t]).wait()
+
+        parts_sent(1, length)
+
+        @pl.when(lead)
+        def _():
+            parts_sent(0, n - 1)
+
+        @pl.when(jnp.logical_not(lead))
+        def _():
+            parts_sent(0, length)
+
         pass_bytes(0, length, send_sem.at[4], start, columns - start)
         pass_bytes(1, length - 1, send_sem.at[5], tail, columns - tail)
         pass_bytes(1, length - 2, send_sem.at[6], 0, tail)
@@ -486,10 +545,12 @@
             pltpu.VMEM((1, rows), jnp.float32),
             pltpu.VMEM((rows, lanes), jnp.float32),
             pltpu.VMEM((n, 2, 1, columns), jnp.float32),
+            pltpu.VMEM((length, 2, 1, columns), jnp.float32),
             pltpu.VMEM((3, rows, chunks[0][2]), jnp.float32),
             pltpu.SemaphoreType.DMA,
             pltpu.SemaphoreType.DMA((count,)),
-            pltpu.SemaphoreType.DMA,
+            pltpu.SemaphoreType.DMA((2,)),
+            pltpu.SemaphoreType.DMA((3,)),
             pltpu.SemaphoreType.DMA((3,)),
             pltpu.SemaphoreType.DMA((11,)),
             pltpu.SemaphoreType.DMA((length, count)),

time: 247 us -> 246 us (level)
  no operation moved by 1% of the time
where the time goes in v4:
time: 246 us
  Pallas kernels  243 us (99%)
    pallas_call x1, Pallas kernels, per_device(): pl.pallas_call(functools.partial(gather_kernel, n), out_shape=(pltpu.VMEM...  234 us
    pallas_call x1, Pallas kernels, write_out(): pl.pallas_call(functools.partial(write_kernel, pieces), out_shape=[jax.Sh...  8.32 us
  transfers between devices with their start and end apart: 2, of which 1 were waited for; matrix products, arithmetic and copies ran while one was open for 0% of the time, Pallas kernels for 3%

profile of v4, /device:TPU:0, one launch (start us, length us, event | category | flops | bytes accessed | tf_op | source)
XLA Modules:
  0.0 245.8 jit_solution(13178866399025029488)
XLA Ops:
  0.6 233.9 %step_and_gather.1 = (bf16[2560,2432]{1,0:T(8,128)(2,1)S(1)}, bf16[2560,2432]{1,0:T(8,128)(2,1)S(1)}, f32[1,2432]{1,0:T(1,128)S(1)}, f32[1,2432]{1,0:T(1,128)S(1...) custom-call(f32[320]{0:T(512)} %gain_ref.1, f32[320,2432]{1,0:T(8,128)} %wg.1, f32[320,2432]{1,0:T(8,128)} %mg.1, ...), custom_call_target="tpu_custom_call" | custom-call | tf_op jit(solution)/shard_map/step_and_gather/pallas_call | solution.py:531
  234.6 0.1 collective-permute-start
  234.7 1.0 collective-permute-start.1
  235.7 8.3 %write_out.1 = (bf16[2560,2432]{1,0:T(8,128)(2,1)}, bf16[2560,2432]{1,0:T(8,128)(2,1)}, f32[2432]{0:T(1024)}, f32[2432]{0:T(1024)}) custom-call(bf16[2560,2432]{1,0:T(8,128)(2,1)S(1)} %get-tuple-element.14.gate, bf16[2560,2432]{1,0:T(8,128)(2,1)S(1)} %get-tuple-element.15.up, f32[1,2432]{1,0:T(1,128)S(1)} %get-tuple-element.16.col_gate, ...), custom_call_target="tpu_custom_call" | custom-call | flops 100000000 | bytes 24903680 | tf_op jit(solution)/shard_map/write_out/pallas_call | solution.py:478
  244.0 0.8 collective-permute-done.from_line
  244.8 0.0 collective-permute-done.1.from_side
  244.8 1.0 place_tails.1
Async XLA Ops:
  234.6 10.2 %collective-permute-start = (bf16[320,896]{1,0:T(8,128)(2,1)}, bf16[320,896]{1,0:T(8,128)(2,1)S(1)}, u32[]{:S(2)}, u32[]{:S(2)}) collective-permute-start(bf16[320,896]{1,0:T(8,128)(2,1)} %get-tuple-element.20), channel_id=1, source_target_pairs={{0,8},{4,12},{8,0},{12,4},{16,24},{20,28},{24,16},{28,20},{1,9},{5... | collective-permute-start | bytes 1720328 | tf_op jit(solution)/shard_map/ppermute | solution.py:570
  234.7 10.1 %collective-permute-start.1 = (bf16[320,896]{1,0:T(8,128)(2,1)}, bf16[320,896]{1,0:T(8,128)(2,1)S(1)}, u32[]{:S(2)}, u32[]{:S(2)}) collective-permute-start(bf16[320,896]{1,0:T(8,128)(2,1)} %get-tuple-element.21), channel_id=1, source_target_pairs={{0,4},{4,0},{8,12},{12,8},{16,20},{20,16},{24,28},{28,24},{1,5},{5... | collective-permute-start | bytes 1720328 | tf_op jit(solution)/shard_map/ppermute | solution.py:571
